TPU v7x, 256 devices: a whole 4x4x8 slice. The times are simulated.
256 devices in a mesh: tbl: 64 (over y, z, core), pair: 4 (over x).
Axes of the slice: x: 4, y: 4, z: 8, core: 2. Of those that a mesh axis runs over, the one named last changes fastest.
Arguments:
- codes: bfloat16 [128, 64, 131072], P('tbl', None, 'pair'), may hold values from -127 to 127
- scales: float32 [128, 131072], P('tbl', 'pair'), may hold values from 0.002 to 0.02
- shard_slot: int32 [64, 2], replicated, may hold values from -1 to 53, as said below
- weight_first: bfloat16 [351, 1024], replicated, may hold values from -0.3125 to 0.3125
- bias_first: float32 [1024], replicated, may hold values from -3 to 3
- weight_second: bfloat16 [1024, 1024], replicated, may hold values from -0.1875 to 0.1875
- bias_second: float32 [1024], replicated, may hold values from -3 to 3
- weight_third: bfloat16 [1024, 512], replicated, may hold values from -0.1875 to 0.1875
- bias_third: float32 [512], replicated, may hold values from -3 to 3
- weight_fourth: bfloat16 [512, 256], replicated, may hold values from -0.25 to 0.25
- bias_fourth: float32 [256], replicated, may hold values from -3 to 3
- weight_out: bfloat16 [256], replicated, may hold values from -0.375 to 0.375
- bias_out: float32 [1], replicated, may hold values from -3 to 3
Outputs:
- logits: float32 [4, 32768], P(None, 'tbl')
Inputs may be any that keep to these rules, and one draw needn't show every extreme that they name: `shard_slot`: each shard 0 to 53 stands in exactly one slot; all other slots hold -1. For k below half of the tbl size, row k holds its shards in its first slots and the row half the tbl size further holds its shards in its last slots, and the two rows hold 2 shards or fewer together. Some row holds 2 shards.
All inputs are finite; a program needn't handle non-finite values.
Results may differ from a plain program's by a relative error of at most 0.03.
Values may be sent and summed in bfloat16 or wider, within the bound.
A program may use at most 128 MiB of HBM per device.

v0:
```python
import jax
import jax.numpy as jnp
import numpy as np
from jax import lax
from jax.sharding import PartitionSpec as P

TABLES = 27


def copy_for_each(array, axis):
    copies = jnp.broadcast_to(array, (lax.axis_size(axis), *array.shape))
    return lax.all_to_all(copies, axis, split_axis=0, concat_axis=0, tiled=True)


def in_order(pieces, dim):
    pieces = jnp.moveaxis(pieces, 0, dim)
    lengths = pieces.shape
    return pieces.reshape(*lengths[:dim], lengths[dim] * lengths[dim + 1], *lengths[dim + 2 :])


def gather_directly(array, axis, dim):
    pieces = copy_for_each(array, axis)
    return in_order(pieces, dim)


def pair_columns(tables):
    first, second = np.triu_indices(tables, 1)
    return (first * tables + second).astype(np.int32)


def shard_positions(slot_table, shard_total):
    flat = slot_table.reshape(-1)
    matches = flat[None, :] == jnp.arange(shard_total, dtype=jnp.int32)[:, None]
    places = jnp.arange(flat.shape[0], dtype=jnp.int32)[None, :]
    return jnp.sum(jnp.where(matches, places, 0), axis=1)


def dense_layer(inputs, weight, bias):
    product = jnp.dot(
        inputs.astype(jnp.float32), weight.astype(jnp.float32), precision=lax.Precision.HIGHEST
    )
    return jax.nn.relu(product + bias).astype(jnp.bfloat16)


def score_samples(picked_codes, picked_scales, layers):
    table_count = picked_codes.shape[0] // 2
    column_count = picked_codes.shape[1]
    count = picked_codes.shape[2]
    halves = picked_codes.reshape(table_count, 2, column_count, count)
    half_scales = picked_scales.reshape(table_count, 2, count)
    gram = jnp.zeros((count, table_count, table_count), jnp.float32)
    for part_index in range(2):
        block_codes = halves[:, part_index].astype(jnp.float32)
        products = jnp.einsum(
            "icb,jcb->bij", block_codes, block_codes, precision=lax.Precision.HIGHEST
        )
        factor = half_scales[:, part_index]
        outer = jnp.transpose(factor)[:, :, None] * jnp.transpose(factor)[:, None, :]
        gram = gram + products * outer
    flat = gram.reshape(count, table_count * table_count)
    hidden = flat[:, pair_columns(table_count)].astype(jnp.bfloat16)
    for weight, bias in layers[:-1]:
        hidden = dense_layer(hidden, weight, bias)
    weight_last, bias_last = layers[-1]
    final = jnp.dot(
        hidden.astype(jnp.float32), weight_last.astype(jnp.float32), precision=lax.Precision.HIGHEST
    )
    return final + bias_last[0]


def per_device(
    codes,
    scales,
    shard_slot,
    weight_first,
    bias_first,
    weight_second,
    bias_second,
    weight_third,
    bias_third,
    weight_fourth,
    bias_fourth,
    weight_out,
    bias_out,
):
    layers = (
        (weight_first, bias_first),
        (weight_second, bias_second),
        (weight_third, bias_third),
        (weight_fourth, bias_fourth),
        (weight_out, bias_out),
    )
    slot_count = codes.shape[0]
    column_count = codes.shape[1]
    tbl_count = lax.axis_size("tbl")
    batch_local = codes.shape[2] // tbl_count
    shard_total = 2 * TABLES

    def make_scorer(positions):

        def scorer(received):
            got_codes, got_scales = received
            picked_codes = jnp.take(got_codes[:, :, 0, :], positions, axis=0)
            picked_scales = jnp.take(got_scales[:, 0, 0, :], positions, axis=0)
            return score_samples(picked_codes, picked_scales, layers)

        return scorer

    packed_codes = codes.reshape(slot_count, column_count, tbl_count, batch_local)
    packed_scales = scales.reshape(slot_count, 1, tbl_count, batch_local)
    scorer = make_scorer(shard_positions(shard_slot, shard_total))
    logits = scorer(
        (
            lax.all_to_all(packed_codes, "tbl", split_axis=2, concat_axis=0, tiled=True),
            lax.all_to_all(
                packed_scales.astype(jnp.bfloat16), "tbl", split_axis=2, concat_axis=0, tiled=True
            ).astype(packed_scales.dtype),
        )
    )
    return gather_directly(logits[None, :], "pair", 0)


def solution(mesh):
    return jax.shard_map(
        per_device,
        mesh=mesh,
        in_specs=(
            P("tbl", None, "pair"),
            P("tbl", "pair"),
            P(),
            P(),
            P(),
            P(),
            P(),
            P(),
            P(),
            P(),
            P(),
            P(),
            P(),
        ),
        out_specs=P(None, "tbl"),
        check_vma=False,
    )
```

profile of v0, /device:TPU:1, one launch (start us, length us, event | category | flops | bytes accessed | tf_op | source)
XLA Modules:
  0.0 282.7 jit_solution(4032717320635290374)
XLA Ops:
  0.0 0.0 copy-start
  0.0 1.8 convert_element_type.56
  1.8 13.1 %all-to-all-start.1 = ((bf16[2,1,64,512]{3,0,1,2:T(2,128)(2,1)}), bf16[2,1,64,512]{3,0,1,2:T(2,128)(2,1)S(1)}, u32[]{:S(2)}, u32[]{:S(2)}) async-start(bf16[2,1,64,512]{3,0,1,2:T(2,128)(2,1)} %bitcast.7), calls=%async_computation.1 | async-start | bytes 262144 | tf_op jit(solution)/shard_map/all_to_all | solution.py:115
  15.0 7.9 %copy.56 = bf16[2,8,64,8,512]{4,3,1,0,2:T(8,128)(2,1)} copy(bf16[2,8,64,8,512]{4,3,2,1,0:T(8,128)(2,1)} %bitcast.56) | data formatting | bytes 16777216 | tf_op jit(solution)/shard_map/reshape | solution.py:109
  22.9 2.4 all-to-all-done.1
  25.3 0.0 copy-start.3
  25.3 0.0 copy-start.10
  25.3 8.2 %all-to-all-start = ((bf16[2,64,64,512]{3,1,0,2:T(8,128)(2,1)}), bf16[2,64,64,512]{3,1,0,2:T(8,128)(2,1)}, u32[]{:S(2)}, u32[]{:S(2)}) async-start(bf16[2,64,64,512]{3,1,0,2:T(8,128)(2,1)} %bitcast.54), calls=%async_computation | async-start | bytes 16777216 | tf_op jit(solution)/shard_map/all_to_all | solution.py:114
  33.6 0.0 copy-done.3
  33.6 0.1 copy.44
  33.7 0.1 eq.15
  33.8 0.1 select_reduce_fusion
  33.9 0.1 reduce_sum.14
  34.1 0.1 copy.45
  34.2 0.0 copy-done.10
  34.9 0.0 copy-done.2
  34.9 0.1 convert_bitcast_fusion
  35.0 0.2 reshape.72
  35.2 0.6 gather_fusion.1
  35.8 0.1 gather.18
  35.9 0.2 copy.49
  36.2 183.1 %all-to-all-done = bf16[2,64,64,512]{3,1,0,2:T(8,128)(2,1)} async-done(((bf16[2,64,64,512]{3,1,0,2:T(8,128)(2,1)}), bf16[2,64,64,512]{3,1,0,2:T(8,128)(2,1)}, u32[]{:S(2)}, u32[]{:S(2)}) %all-to-all-start) | async-done | bytes 8388640 | tf_op jit(solution)/shard_map/all_to_all | solution.py:114
  219.3 6.0 %gather_fusion = bf16[54,64,512]{2,1,0:T(8,128)(2,1)} fusion(bf16[128,64,512]{2,1,0:T(8,128)(2,1)} %bitcast.2, s32[1024]{0:T(1024)S(1)} %pad_clamp_fusion.1), kind=kCustom, calls=%fused_computation | custom fusion | bytes 7078104 | tf_op jit(solution)/shard_map/jit(_take)/gather | solution.py:103
  225.3 13.0 %copy.47 = bf16[27,2,64,512]{2,0,3,1:T(8,128)(2,1)} copy(bf16[27,2,64,512]{3,2,1,0:T(8,128)(2,1)} %bitcast.55) | data formatting | bytes 7077888 | tf_op jit(solution)/shard_map/jit(_take)/gather | solution.py:103
  238.4 7.4 %broadcast_select_fusion = bf16[27,2,64,512]{2,0,3,1:T(8,128)(2,1)} fusion(bf16[27,2,64,512]{2,0,3,1:T(8,128)(2,1)} %copy.47, pred[27,2]{0,1:T(4,128)(4,1)S(1)} %copy.45), kind=kLoop, calls=%fused_computation.5 | loop fusion | flops 1769472 | bytes 7077942 | tf_op jit(solution)/shard_map/jit(_take)/select_n | solution.py:103
  245.8 5.9 %fusion = f32[512,27,27]{2,1,0:T(8,128)S(1)} fusion(bf16[27,2,64,512]{2,0,3,1:T(8,128)(2,1)} %broadcast_select_fusion), kind=kOutput, calls=%fused_computation.7 | convolution fusion | flops 47775744 | bytes 5687296 | tf_op jit(solution)/shard_map/icb,jcb->bij/dot_general | solution.py:54
  251.6 0.0 copy-done.1
  251.7 6.7 %multiply_add_fusion = bf16[512,27,27]{2,1,0:T(8,128)(2,1)} fusion(f32[512,27,27]{2,1,0:T(8,128)S(1)} %fusion, f32[512,27]{1,0:T(8,128)S(1)} %get-tuple-element.6, f32[512,27]{1,0:T(8,128)S(1)} %get-tuple-element.5, bf16[27,2,64,512]{2,0,3,1:T(8,128)(2,1)S(1)} %copy-done.1), kind=kOutput, calls=%fused_computation.4 | convolution fusion | flops 50015232 | bytes 14377984 | tf_op jit(solution)/shard_map/icb,jcb->bij/dot_general | solution.py:54
  258.4 7.7 %reshape.100 = bf16[512,729]{1,0:T(8,128)(2,1)} reshape(bf16[512,27,27]{2,1,0:T(8,128)(2,1)} %multiply_add_fusion) | data formatting | bytes 1492992 | tf_op jit(solution)/shard_map/reshape | solution.py:60
  266.1 1.4 copy.51
  267.5 0.0 copy-start.5
  267.6 0.0 copy-start.9
  267.6 2.0 gather_fusion.2
  269.6 0.0 copy-done.6
  269.6 0.0 copy-start.4
  269.6 1.9 maximum_convert_fusion.1
  271.6 0.0 copy-done
  271.6 0.0 copy-done.7
  271.6 1.3 maximum_convert_fusion
  272.9 0.0 copy-done.8
  272.9 0.0 copy-done.4
  272.9 0.7 fusion.3
  273.6 0.0 copy-done.5
  273.6 0.0 copy-done.9
  273.6 0.3 fusion.5
  273.9 0.2 fusion.8
  274.1 8.0 %all_to_all.29 = f32[4,1,512]{2,1,0:T(1,128)S(1)} all-to-all(f32[4,1,512]{2,1,0:T(1,128)S(1)} %broadcast_in_dim.56), channel_id=1, replica_groups=mesh['tbl'=64,'pair'=4] {'pair'}, dimensions={0} | all-to-all | bytes 16384 | tf_op jit(solution)/shard_map/all_to_all | solution.py:12
  282.1 0.6 copy.57
  (14 shorter events, 0.1 us)
Async XLA Ops:
  0.0 271.6 %copy-start = (bf16[1024,1024]{1,0:T(8,128)(2,1)S(1)}, bf16[1024,1024]{1,0:T(8,128)(2,1)}, u32[]{:S(2)}) copy-start(bf16[1024,1024]{1,0:T(8,128)(2,1)} %param.20) | copy-start | bytes 6291460
  1.8 23.5 %all-to-all-start.1 = ((bf16[2,1,64,512]{3,0,1,2:T(2,128)(2,1)}), bf16[2,1,64,512]{3,0,1,2:T(2,128)(2,1)S(1)}, u32[]{:S(2)}, u32[]{:S(2)}) async-start(bf16[2,1,64,512]{3,0,1,2:T(2,128)(2,1)} %bitcast.7), calls=%async_computation.1 | async-start | bytes 262144 | tf_op jit(solution)/shard_map/all_to_all | solution.py:115
  25.3 8.3 %copy-start.3 = (s32[64,2]{0,1:T(2,128)S(1)}, s32[64,2]{0,1:T(2,128)}, u32[]{:S(2)}) copy-start(s32[64,2]{0,1:T(2,128)} %param.17) | copy-start | bytes 1540
  25.3 8.8 %copy-start.10 = (bf16[256]{0:T(256)(128)(2,1)S(1)}, bf16[256]{0:T(256)(128)(2,1)}, u32[]{:S(2)}) copy-start(bf16[256]{0:T(256)(128)(2,1)} %param.26) | copy-start | bytes 1540
  25.3 9.5 %copy-start.2 = (s32[351]{0:T(512)S(1)}, s32[351]{0:T(512)}, u32[]{:S(2)}) copy-start(s32[351]{0:T(512)} %constant.49) | copy-start | bytes 4216
  25.3 194.0 %all-to-all-start = ((bf16[2,64,64,512]{3,1,0,2:T(8,128)(2,1)}), bf16[2,64,64,512]{3,1,0,2:T(8,128)(2,1)}, u32[]{:S(2)}, u32[]{:S(2)}) async-start(bf16[2,64,64,512]{3,1,0,2:T(8,128)(2,1)} %bitcast.54), calls=%async_computation | async-start | bytes 16777216 | tf_op jit(solution)/shard_map/all_to_all | solution.py:114
  245.8 5.9 %copy-start.1 = (bf16[27,2,64,512]{2,0,3,1:T(8,128)(2,1)S(1)}, bf16[27,2,64,512]{2,0,3,1:T(8,128)(2,1)}, u32[]{:S(2)}) copy-start(bf16[27,2,64,512]{2,0,3,1:T(8,128)(2,1)} %broadcast_select_fusion) | copy-start | bytes 10616836
  258.4 11.2 %copy-start.6 = (f32[1024]{0:T(1024)S(1)}, f32[1024]{0:T(1024)}, u32[]{:S(2)}) copy-start(f32[1024]{0:T(1024)} %param.19) | copy-start | bytes 12292
  258.4 13.2 %copy-start.7 = (f32[1024]{0:T(1024)S(1)}, f32[1024]{0:T(1024)}, u32[]{:S(2)}) copy-start(f32[1024]{0:T(1024)} %param.21) | copy-start | bytes 12292
  266.1 6.7 %copy-start.8 = (f32[512]{0:T(512)S(1)}, f32[512]{0:T(512)}, u32[]{:S(2)}) copy-start(f32[512]{0:T(512)} %param.23) | copy-start | bytes 6148
  267.5 6.1 %copy-start.5 = (bf16[512,256]{1,0:T(8,128)(2,1)S(1)}, bf16[512,256]{1,0:T(8,128)(2,1)}, u32[]{:S(2)}) copy-start(bf16[512,256]{1,0:T(8,128)(2,1)} %param.24) | copy-start | bytes 786436
  267.6 6.1 %copy-start.9 = (f32[256]{0:T(256)S(1)}, f32[256]{0:T(256)}, u32[]{:S(2)}) copy-start(f32[256]{0:T(256)} %param.25) | copy-start | bytes 3076
  269.6 3.3 %copy-start.4 = (bf16[1024,512]{1,0:T(8,128)(2,1)S(1)}, bf16[1024,512]{1,0:T(8,128)(2,1)}, u32[]{:S(2)}) copy-start(bf16[1024,512]{1,0:T(8,128)(2,1)} %param.22) | copy-start | bytes 3145732
where the time goes:
time: 283 us
  waiting for transfers between devices  186 us (66%)
  local copies, waits for them, and re-layouts  40.4 us (14%)
  starting transfers between devices  21.4 us (8%)
  matrix products  17 us (6%)
  other arithmetic  9.51 us (3%)
  blocking collectives  7.98 us (3%)
    all_to_all x1, waiting for transfers between devices, per_device(): lax.all_to_all(packed_codes, 'tbl', split_axis=2, concat_axis=0, tiled=True)  183 us
    gather x2, local copies, waits for them, and re-layouts, scorer(): picked_codes = jnp.take(got_codes[:, :, 0, :], positions, axis=0)  19.1 us
    all_to_all x1, starting transfers between devices, per_device(): lax.all_to_all(packed_scales.astype(jnp.bfloat16), 'tbl', split_axis=2, c...  13.1 us
    dot_general x2, matrix products, score_samples(): jnp.einsum('icb,jcb->bij', block_codes, block_codes, precision=lax.Precis...  12.6 us
    reshape x2, local copies, waits for them, and re-layouts, score_samples(): flat = gram.reshape(count, table_count * table_count)  9.14 us
    all_to_all x1, starting transfers between devices, per_device(): lax.all_to_all(packed_codes, 'tbl', split_axis=2, concat_axis=0, tiled=True)  8.24 us
    all_to_all x1, blocking collectives, copy_for_each(): return lax.all_to_all(copies, axis, split_axis=0, concat_axis=0, tiled=True)  7.98 us
    reshape x1, local copies, waits for them, and re-layouts, per_device(): codes.reshape(slot_count, column_count, tbl_count, batch_local)  7.9 us
  transfers between devices with their start and end apart: 2, of which 2 were waited for; matrix products, arithmetic and copies ran while one was open for 3% of the time, Pallas kernels for 0%

commit v1 on v0

v1 whole, which is shorter than its diff:
```python
import functools

import jax
import jax.numpy as jnp
from jax import lax
from jax.experimental import pallas as pl
from jax.experimental.pallas import tpu as pltpu
from jax.sharding import PartitionSpec as P

MESH = pl.DeviceIdType.MESH
F32 = jnp.float32
BF16 = jnp.bfloat16

TABLES = 27
SHIFTS = TABLES // 2
PAIRS = TABLES * SHIFTS
NY, NZC, NX = 4, 16, 4
NQ, NG = 4, 4
CHUNKS = NQ * NG
AHEAD = 4
LAG = 2
Z_ORDER = (4, 3, 5, 2, 6, 1, 7)


def kernel(
    slot_ref,
    place_ref,
    bout_ref,
    codes,
    scales,
    w1,
    b1,
    w2,
    b2,
    w3,
    b3,
    w4,
    b4,
    wout_ref,
    out_ref,
    y_recv,
    merged,
    z_recv,
    sc_in,
    sc_send,
    y_sc,
    m_sc,
    z_sc,
    sc,
    unit,
    vals,
    acc,
    xt,
    lg,
    w1v,
    w1p,
    b1v,
    w2v,
    b2v,
    w3v,
    b3v,
    w4v,
    b4v,
    y_ssem,
    y_rsem,
    z_ssem,
    z_rsem,
    sc_ssem,
    sc_rsem,
    lg_ssem,
    lg_rsem,
    in_sem,
    w_sem,
):
    me = lax.axis_index("tbl")
    px = lax.axis_index("pair")
    y = me // NZC
    zc = me % NZC
    z = zc // 2
    core = zc % 2

    sc_load = pltpu.make_async_copy(scales, sc_in, in_sem)
    sc_load.start()
    weights = ((w1, w1v), (b1, b1v), (w2, w2v), (b2, b2v), (w3, w3v), (b3, b3v), (w4, w4v), (b4, b4v))
    loads = [pltpu.make_async_copy(src, dst, w_sem.at[i]) for i, (src, dst) in enumerate(weights)]
    for load in loads:
        load.start()

    y_peers = [((y + k) % NY) for k in (1, 3, 2)]
    z_peers = [((z + dz) % 8) * 2 + c for dz in Z_ORDER for c in range(2)] + [z * 2 + (1 - core)]
    x_peers = [((px + k) % NX) for k in (1, 3, 2)]

    barrier = pltpu.get_barrier_semaphore()
    for peer in y_peers:
        pl.semaphore_signal(barrier, inc=1, device_id={"tbl": peer * NZC + zc}, device_id_type=MESH)
    for peer in z_peers:
        pl.semaphore_signal(barrier, inc=1, device_id={"tbl": y * NZC + peer}, device_id_type=MESH)
    for peer in x_peers:
        pl.semaphore_signal(barrier, inc=1, device_id={"pair": peer}, device_id_type=MESH)
    pl.semaphore_wait(barrier, len(y_peers) + len(z_peers) + len(x_peers))

    def send_y(ch):
        q = ch // NG
        g = ch % NG
        for peer in y_peers:
            pltpu.make_async_remote_copy(
                src_ref=codes.at[:, pl.ds(g * 2, 2), pl.ds(peer * NZC, NZC), q],
                dst_ref=y_recv.at[ch, y],
                send_sem=y_ssem.at[ch],
                recv_sem=y_rsem.at[ch],
                device_id={"tbl": peer * NZC + zc},
                device_id_type=MESH,
            ).start()
        pltpu.make_async_copy(
            codes.at[:, pl.ds(g * 2, 2), pl.ds(y * NZC, NZC), q], y_recv.at[ch, y], y_rsem.at[ch]
        ).start()

    send_y(0)

    sc_load.wait()
    sc_send[...] = sc_in[...].reshape(NY * 8, 16, 128).astype(BF16)
    y_sc[y] = sc_send[pl.ds(y * 8, 8)]
    for peer in y_peers:
        pltpu.make_async_remote_copy(
            src_ref=sc_send.at[pl.ds(peer * 8, 8)],
            dst_ref=y_sc.at[y],
            send_sem=sc_ssem.at[0],
            recv_sem=sc_rsem.at[0],
            device_id={"tbl": peer * NZC + zc},
            device_id_type=MESH,
        ).start()
    for ch in range(1, AHEAD):
        send_y(ch)

    for load in loads:
        load.wait()
    row = lax.broadcasted_iota(jnp.int32, (SHIFTS * 32, PAIRS), 0)
    col = lax.broadcasted_iota(jnp.int32, (SHIFTS * 32, PAIRS), 1)
    first = row % 32
    second = first + row // 32 + 1
    second = jnp.where(second >= TABLES, second - TABLES, second)
    low = jnp.minimum(first, second)
    high = jnp.maximum(first, second)
    rank = low * TABLES - (low * (low + 1)) // 2 + high - low - 1
    chosen = jnp.where((rank == col) & (first < TABLES), 1.0, 0.0).astype(BF16)
    w1p[...] = jnp.dot(chosen, w1v[...], preferred_element_type=F32).astype(BF16)
    xt[...] = jnp.zeros_like(xt)
    acc[...] = jnp.zeros_like(acc)

    flags = [[slot_ref[((p * NZC) + zc) * 2 + j] for j in range(2)] for p in range(2)]

    def merge(ch):
        pltpu.make_async_copy(y_recv.at[ch], y_recv.at[ch], y_rsem.at[ch]).wait()
        for p in range(2):
            for j in range(2):
                take_low = flags[p][j] >= 0
                for g in range(2):
                    merged[ch, :, p, j, g] = jnp.where(take_low, y_recv[ch, p, j, g], y_recv[ch, p + 2, j, g])
        for peer in z_peers:
            pltpu.make_async_remote_copy(
                src_ref=merged.at[ch, peer],
                dst_ref=z_recv.at[ch, zc],
                send_sem=z_ssem.at[ch],
                recv_sem=z_rsem.at[ch],
                device_id={"tbl": y * NZC + peer},
                device_id_type=MESH,
            ).start()
        z_recv[ch, zc] = merged[ch, zc]

    def merge_scales():
        pltpu.make_async_copy(y_sc.at[pl.ds(0, 3)], y_sc.at[pl.ds(0, 3)], sc_rsem.at[0]).wait()
        odd = lax.broadcasted_iota(jnp.int32, (8, 16, 128), 1) % 2
        picked = []
        for p in range(2):
            mask = jnp.where(odd == 0, flags[p][0], flags[p][1]) >= 0
            picked.append(jnp.where(mask, y_sc[p].astype(F32), y_sc[p + 2].astype(F32)))
        for c in range(2):
            both = jnp.concatenate([part[:, c * 8 : c * 8 + 8] for part in picked], axis=1)
            m_sc[:, c] = both.astype(BF16)
        for peer in z_peers:
            pltpu.make_async_remote_copy(
                src_ref=m_sc.at[peer // 2, peer % 2],
                dst_ref=z_sc.at[zc],
                send_sem=sc_ssem.at[1],
                recv_sem=sc_rsem.at[1],
                device_id={"tbl": y * NZC + peer},
                device_id_type=MESH,
            ).start()
        z_sc[zc] = m_sc[z, core]

    def spread_scales():
        pltpu.make_async_copy(z_sc.at[pl.ds(0, NZC - 1)], z_sc.at[pl.ds(0, NZC - 1)], sc_rsem.at[1]).wait()

        def body(s, carry):
            rows = z_sc[s].astype(F32)
            for p in range(2):
                for q in range(NQ):
                    for j in range(2):
                        r = p * 8 + q * 2 + j
                        sc[q * 64 + s * 4 + p * 2 + j] = jnp.broadcast_to(rows[r : r + 1], (8, 128))
            return carry

        lax.fori_loop(0, NZC, body, 0)

    def gram(ch):
        q = ch // NG
        pltpu.make_async_copy(z_recv.at[ch, pl.ds(0, NZC - 1)], z_recv.at[ch, pl.ds(0, NZC - 1)], z_rsem.at[ch]).wait()

        def widen(s, carry):
            unit[pl.ds(s * 4, 4)] = z_recv[ch, s].reshape(4, 2, 8, 128).astype(F32)
            return carry

        lax.fori_loop(0, NZC, widen, 0)

        def place(t, carry, again):
            for h in range(2):
                at = place_ref[t * 2 + h]
                factor = sc[q * 64 + at]
                both = unit[at]
                for g in range(2):
                    value = both[g] * factor
                    vals[h * 2 + g, t] = value
                    if again:
                        vals[h * 2 + g, t + TABLES] = value
            return carry

        lax.fori_loop(0, SHIFTS, functools.partial(place, again=True), 0)
        lax.fori_loop(SHIFTS, TABLES, functools.partial(place, again=False), 0)

        def shift(d, carry):
            for b in range(0, TABLES, 9):
                total = acc[d, b : b + 9]
                for k in range(4):
                    total = total + vals[k, b : b + 9] * vals[k, pl.ds(d + 1 + b, 9)]
                acc[d, b : b + 9] = total
            return carry

        lax.fori_loop(0, SHIFTS, shift, 0)

    def layer(inputs, weight, bias):
        product = jnp.dot(inputs, weight[...], preferred_element_type=F32)
        return jnp.maximum(product + bias[...], 0.0).astype(BF16)

    def finish(q):
        def fold(d, carry):
            xt[pl.ds(pl.multiple_of(d * 32, 32), TABLES)] = jnp.sum(acc[d], axis=1)
            acc[d] = jnp.zeros((TABLES, 8, 128), F32)
            return carry

        lax.fori_loop(0, SHIFTS, fold, 0)
        hidden = xt[...].T.astype(BF16)
        hidden = layer(hidden, w1p, b1v)
        hidden = layer(hidden, w2v, b2v)
        hidden = layer(hidden, w3v, b3v)
        hidden = layer(hidden, w4v, b4v)
        last = jnp.broadcast_to(wout_ref[...].astype(F32), (8, 256)).astype(BF16)
        final = lax.dot_general(last, hidden, (((1,), (1,)), ((), ())), preferred_element_type=F32)
        lg[px, q] = final + bout_ref[0]
        for peer in x_peers:
            pltpu.make_async_remote_copy(
                src_ref=lg.at[px, q],
                dst_ref=lg.at[px, q],
                send_sem=lg_ssem.at[q],
                recv_sem=lg_rsem.at[q],
                device_id={"pair": peer},
                device_id_type=MESH,
            ).start()

    def step(i, carry):
        @pl.when(i < CHUNKS)
        def _():
            merge(i)

        @pl.when(i + AHEAD < CHUNKS)
        def _():
            send_y(i + AHEAD)

        @pl.when(i == 0)
        def _():
            merge_scales()

        @pl.when(i == LAG)
        def _():
            spread_scales()

        @pl.when(i >= LAG)
        def _():
            gram(i - LAG)

        @pl.when((i >= LAG) & ((i - LAG) % NG == NG - 1))
        def _():
            finish((i - LAG) // NG)

        return carry

    lax.fori_loop(0, CHUNKS + LAG, step, 0)

    def sent(ch, carry):
        three = y_recv.at[ch, pl.ds(0, 3)]
        pltpu.make_async_copy(three, three, y_ssem.at[ch]).wait()
        most = z_recv.at[ch, pl.ds(0, NZC - 1)]
        pltpu.make_async_copy(most, most, z_ssem.at[ch]).wait()
        return carry

    lax.fori_loop(0, CHUNKS, sent, 0)
    pltpu.make_async_copy(y_sc.at[pl.ds(0, 3)], y_sc.at[pl.ds(0, 3)], sc_ssem.at[0]).wait()
    pltpu.make_async_copy(z_sc.at[pl.ds(0, NZC - 1)], z_sc.at[pl.ds(0, NZC - 1)], sc_ssem.at[1]).wait()
    for q in range(NQ):
        three = lg.at[pl.ds(0, 3), q]
        pltpu.make_async_copy(three, three, lg_ssem.at[q]).wait()
        pltpu.make_async_copy(three, three, lg_rsem.at[q]).wait()
    for p in range(NX):
        for q in range(NQ):
            out_ref[p : p + 1, q * 128 : (q + 1) * 128] = lg[p, q, 0:1]


def per_device(codes, scales, shard_slot, w1, b1, w2, b2, w3, b3, w4, b4, wout, bout):
    flat = shard_slot.reshape(-1)
    spot = jnp.arange(flat.shape[0], dtype=jnp.int32)
    half = flat.shape[0] // 2
    merged_spot = spot % half
    row, j = merged_spot // 2, merged_spot % 2
    merged_spot = (row % NZC) * 4 + (row // NZC) * 2 + j
    matches = flat[None, :] == jnp.arange(2 * TABLES, dtype=jnp.int32)[:, None]
    place = jnp.sum(jnp.where(matches, merged_spot[None, :], 0), axis=1).astype(jnp.int32)

    codes = codes.reshape(2, 8, 8, NY * NZC, NQ, 128).transpose(0, 1, 3, 4, 2, 5)
    scales = scales.reshape(2, NY * NZC, NQ, 128).transpose(1, 2, 0, 3).reshape(NY * NZC, 8, 128)

    any_spec = pl.BlockSpec(memory_space=pl.ANY)
    smem = pl.BlockSpec(memory_space=pltpu.SMEM)
    vmem = pl.BlockSpec(memory_space=pltpu.VMEM)
    dma = pltpu.SemaphoreType.DMA
    return pl.pallas_call(
        kernel,
        out_shape=jax.ShapeDtypeStruct((NX, NQ * 128), F32),
        in_specs=[smem, smem, smem] + [any_spec] * 10 + [vmem],
        out_specs=vmem,
        scratch_shapes=[
            pltpu.VMEM((CHUNKS, NY, 2, 2, NZC, 8, 128), BF16),
            pltpu.VMEM((CHUNKS, NZC, 2, 2, 2, 8, 128), BF16),
            pltpu.VMEM((CHUNKS, NZC, 2, 2, 2, 8, 128), BF16),
            pltpu.VMEM((NY * NZC, 8, 128), F32),
            pltpu.VMEM((NY * 8, 16, 128), BF16),
            pltpu.VMEM((NY, 8, 16, 128), BF16),
            pltpu.VMEM((8, 2, 16, 128), BF16),
            pltpu.VMEM((NZC, 16, 128), BF16),
            pltpu.VMEM((NQ * 64, 8, 128), F32),
            pltpu.VMEM((64, 2, 8, 128), F32),
            pltpu.VMEM((4, TABLES + SHIFTS, 8, 128), F32),
            pltpu.VMEM((SHIFTS, TABLES, 8, 128), F32),
            pltpu.VMEM((SHIFTS * 32, 128), F32),
            pltpu.VMEM((NX, NQ, 8, 128), F32),
            pltpu.VMEM(w1.shape, BF16),
            pltpu.VMEM((SHIFTS * 32, w1.shape[1]), BF16),
            pltpu.VMEM((1, b1.shape[0]), F32),
            pltpu.VMEM(w2.shape, BF16),
            pltpu.VMEM((1, b2.shape[0]), F32),
            pltpu.VMEM(w3.shape, BF16),
            pltpu.VMEM((1, b3.shape[0]), F32),
            pltpu.VMEM(w4.shape, BF16),
            pltpu.VMEM((1, b4.shape[0]), F32),
            dma((CHUNKS,)),
            dma((CHUNKS,)),
            dma((CHUNKS,)),
            dma((CHUNKS,)),
            dma((2,)),
            dma((2,)),
            dma((NQ,)),
            dma((NQ,)),
            dma,
            dma((8,)),
        ],
        compiler_params=pltpu.CompilerParams(
            collective_id=0, has_side_effects=True, vmem_limit_bytes=56 * 1024 * 1024
        ),
    )(flat, place, bout, codes, scales, w1, b1[None], w2, b2[None], w3, b3[None], w4, b4[None], wout[None])


def solution(mesh):
    return jax.shard_map(
        per_device,
        mesh=mesh,
        in_specs=(P("tbl", None, "pair"), P("tbl", "pair")) + (P(),) * 11,
        out_specs=P(None, "tbl"),
        check_vma=False,
    )
```

time: 283 us -> 125 us (0.44)
  waiting for transfers between devices: 186 us -> 0 us
  Pallas kernels: 0 us -> 120 us
  local copies, waits for them, and re-layouts: 40.4 us -> 3.42 us
  starting transfers between devices: 21.4 us -> 0 us
  matrix products: 17 us -> 0 us
  other arithmetic: 9.51 us -> 0.67 us
  blocking collectives: 7.98 us -> 0 us
    all_to_all x2 -> x0, waiting for transfers between devices: 186 us -> none  [the longest x1 183 us: per_device(): lax.all_to_all(packed_codes, 'tbl', split_axis=2, concat_axis=0, tiled=True)]
    pallas_call x0 -> x1, Pallas kernels: none -> 120 us  [per_device(): pl.pallas_call(kernel, out_shape=jax.ShapeDtypeStruct((NX, NQ * 128), F32...]
    gather x6 -> x0, local copies, waits for them, and re-layouts: 22 us -> none  [the longest x2 19.1 us: scorer(): picked_codes = jnp.take(got_codes[:, :, 0, :], positions, axis=0)]
    all_to_all x2 -> x0, starting transfers between devices: 21.4 us -> none  [the longest x1 13.1 us: per_device(): lax.all_to_all(packed_scales.astype(jnp.bfloat16), 'tbl', split_axis=2, c...]
    dot_general x7 -> x0, matrix products: 17 us -> none  [the longest x2 12.6 us: score_samples(): jnp.einsum('icb,jcb->bij', block_codes, block_codes, precision=lax.Precis...]
    reshape x3 -> x1, local copies, waits for them, and re-layouts: 17 us -> 0.14 us  [per_device(): flat = shard_slot.reshape(-1)]
    all_to_all x1 -> x0, blocking collectives: 7.98 us -> none  [copy_for_each(): return lax.all_to_all(copies, axis, split_axis=0, concat_axis=0, tiled=True)]
    select_n x3 -> x0, other arithmetic: 7.44 us -> none  [the longest x2 7.4 us: scorer(): picked_codes = jnp.take(got_codes[:, :, 0, :], positions, axis=0)]
  transfers between devices with their start and end apart: 2 -> 0, of which waited for: 2 -> 0; matrix products, arithmetic and copies ran while one was open for 3% -> 0% of each run, Pallas kernels for 0% -> 0%
where the time goes in v1:
time: 125 us
  Pallas kernels  120 us (96%)
  local copies, waits for them, and re-layouts  3.42 us (3%)
    pallas_call x1, Pallas kernels, per_device(): pl.pallas_call(kernel, out_shape=jax.ShapeDtypeStruct((NX, NQ * 128), F32...  120 us

profile of v1, /device:TPU:1, one launch (start us, length us, event | category | flops | bytes accessed | tf_op | source)
XLA Modules:
  0.0 125.0 jit_solution(7647150213237233904)
XLA Ops:
  0.0 0.8 copy.18
  0.8 0.1 reshape.78.slot_ref
  0.9 0.0 copy-start
  0.9 0.7 select_reduce_fusion.place_ref
  1.6 1.2 broadcast_in_dim.35.wout_ref
  3.5 0.0 copy-done
  3.5 120.2 %shard_map.127 = f32[4,512]{1,0:T(4,128)} custom-call(s32[128]{0:T(128)} %copy-done, s32[54]{0:T(128)} %select_reduce_fusion.place_ref, f32[1]{0:T(128)S(6)} %copy.21.bout_ref, bf16[2,8,64,4,8,128]{5,4,3,2,1,0:T(8,128)(2,1)} %bitcast.12, f32[64,8,128]{2,1,0:T(8,128)} %bitcast.13, bf16[351,1024]{1,0:T(8,128)(2,1)} %w1.1, f32[1,1024]{1,0:T(1,128)} %bitcast.14, ...), custom_call_target="tpu_custom_call" | custom-call | tf_op jit(solution)/shard_map/pallas_call | solution.py:334
  123.7 1.3 %copy.22 = f32[4,512]{1,0:T(4,128)} copy(f32[4,512]{1,0:T(4,128)} %shard_map.127) | data formatting | bytes 16384
  (1 shorter events, 0.0 us)
Async XLA Ops:
  0.9 2.6 %copy-start = (s32[128]{0:T(128)}, s32[128]{0:T(128)S(1)}, u32[]{:S(2)}) copy-start(s32[128]{0:T(128)S(1)} %reshape.78.slot_ref) | copy-start | bytes 1540

commit v2 on v1

--- a/solution.py
+++ b/solution.py
@@ -15,17 +15,17 @@
 SHIFTS = TABLES // 2
 PAIRS = TABLES * SHIFTS
 NY, NZC, NX = 4, 16, 4
-NQ, NG = 4, 4
-CHUNKS = NQ * NG
-AHEAD = 4
-LAG = 2
+NQ, NG = 4, 8
+SPLIT = 1
+J = 2 // SPLIT
+CHUNKS = NQ * NG * SPLIT
+AHEAD = 6 * SPLIT
+LAG = 4 * SPLIT - 1
 Z_ORDER = (4, 3, 5, 2, 6, 1, 7)
 
 
 def kernel(
-    slot_ref,
-    place_ref,
-    bout_ref,
+    slots,
     codes,
     scales,
     w1,
@@ -36,8 +36,13 @@
     b3,
     w4,
     b4,
-    wout_ref,
+    wout,
     out_ref,
+    slot_v,
+    slot_s,
+    place_v,
+    place_s,
+    woutv,
     y_recv,
     merged,
     z_recv,
@@ -70,6 +75,7 @@
     lg_ssem,
     lg_rsem,
     in_sem,
+    slot_sem,
     w_sem,
 ):
     me = lax.axis_index("tbl")
@@ -81,7 +87,13 @@
 
     sc_load = pltpu.make_async_copy(scales, sc_in, in_sem)
     sc_load.start()
-    weights = ((w1, w1v), (b1, b1v), (w2, w2v), (b2, b2v), (w3, w3v), (b3, b3v), (w4, w4v), (b4, b4v))
+    slot_loads = [
+        pltpu.make_async_copy(slots, slot_v, slot_sem.at[0]),
+        pltpu.make_async_copy(slots, slot_s, slot_sem.at[1]),
+    ]
+    for load in slot_loads:
+        load.start()
+    weights = ((w1, w1v), (b1, b1v), (w2, w2v), (b2, b2v), (w3, w3v), (b3, b3v), (w4, w4v), (b4, b4v), (wout, woutv))
     loads = [pltpu.make_async_copy(src, dst, w_sem.at[i]) for i, (src, dst) in enumerate(weights)]
     for load in loads:
         load.start()
@@ -100,11 +112,12 @@
     pl.semaphore_wait(barrier, len(y_peers) + len(z_peers) + len(x_peers))
 
     def send_y(ch):
-        q = ch // NG
-        g = ch % NG
+        q = ch // (NG * SPLIT)
+        g = ch // SPLIT % NG
+        j = ch % SPLIT
         for peer in y_peers:
             pltpu.make_async_remote_copy(
-                src_ref=codes.at[:, pl.ds(g * 2, 2), pl.ds(peer * NZC, NZC), q],
+                src_ref=codes.at[pl.ds(j, J), g, pl.ds(peer * NZC, NZC), q],
                 dst_ref=y_recv.at[ch, y],
                 send_sem=y_ssem.at[ch],
                 recv_sem=y_rsem.at[ch],
@@ -112,7 +125,7 @@
                 device_id_type=MESH,
             ).start()
         pltpu.make_async_copy(
-            codes.at[:, pl.ds(g * 2, 2), pl.ds(y * NZC, NZC), q], y_recv.at[ch, y], y_rsem.at[ch]
+            codes.at[pl.ds(j, J), g, pl.ds(y * NZC, NZC), q], y_recv.at[ch, y], y_rsem.at[ch]
         ).start()
 
     send_y(0)
@@ -147,15 +160,28 @@
     xt[...] = jnp.zeros_like(xt)
     acc[...] = jnp.zeros_like(acc)
 
-    flags = [[slot_ref[((p * NZC) + zc) * 2 + j] for j in range(2)] for p in range(2)]
+    for load in slot_loads:
+        load.wait()
+    shard = lax.broadcasted_iota(jnp.int32, (56, NY * NZC), 0)
+    table_row = lax.broadcasted_iota(jnp.int32, (56, NY * NZC), 1) % (2 * NZC)
+    spot = table_row % NZC * 4 + table_row // NZC * 2
+    place = jnp.zeros((56, 1), jnp.int32)
+    for j in range(2):
+        here = jnp.broadcast_to(slot_v[j : j + 1], shard.shape) == shard
+        found = jnp.max(jnp.where(here, spot + j, 0), axis=1, keepdims=True)
+        place = jnp.maximum(place, found)
+    place_v[...] = jnp.broadcast_to(place, (56, 128))
+    place_copy = pltpu.make_async_copy(place_v, place_s, slot_sem.at[0])
+    place_copy.start()
+    place_copy.wait()
+    flags = [[slot_s[j, p * NZC + zc] for j in range(2)] for p in range(2)]
 
     def merge(ch):
         pltpu.make_async_copy(y_recv.at[ch], y_recv.at[ch], y_rsem.at[ch]).wait()
         for p in range(2):
-            for j in range(2):
-                take_low = flags[p][j] >= 0
-                for g in range(2):
-                    merged[ch, :, p, j, g] = jnp.where(take_low, y_recv[ch, p, j, g], y_recv[ch, p + 2, j, g])
+            for n in range(J):
+                flag = flags[p][n] if SPLIT == 1 else jnp.where(ch % 2 == 0, flags[p][0], flags[p][1])
+                merged[ch, :, p, n] = jnp.where(flag >= 0, y_recv[ch, p, n], y_recv[ch, p + 2, n])
         for peer in z_peers:
             pltpu.make_async_remote_copy(
                 src_ref=merged.at[ch, peer],
@@ -202,40 +228,50 @@
 
         lax.fori_loop(0, NZC, body, 0)
 
-    def gram(ch):
-        q = ch // NG
-        pltpu.make_async_copy(z_recv.at[ch, pl.ds(0, NZC - 1)], z_recv.at[ch, pl.ds(0, NZC - 1)], z_rsem.at[ch]).wait()
+    def gram(n):
+        q = n // NG
+        for part in range(SPLIT):
+            most = z_recv.at[n * SPLIT + part, pl.ds(0, NZC - 1)]
+            pltpu.make_async_copy(most, most, z_rsem.at[n * SPLIT + part]).wait()
 
         def widen(s, carry):
-            unit[pl.ds(s * 4, 4)] = z_recv[ch, s].reshape(4, 2, 8, 128).astype(F32)
+            for half in range(2):
+                for p in range(2):
+                    for j in range(2):
+                        chunk = n if SPLIT == 1 else n * 2 + j
+                        piece = z_recv[chunk, s * 2 + half, p, j if SPLIT == 1 else 0]
+                        unit[s * 8 + half * 4 + p * 2 + j] = piece.astype(F32)
             return carry
 
-        lax.fori_loop(0, NZC, widen, 0)
-
-        def place(t, carry, again):
-            for h in range(2):
-                at = place_ref[t * 2 + h]
-                factor = sc[q * 64 + at]
-                both = unit[at]
-                for g in range(2):
-                    value = both[g] * factor
-                    vals[h * 2 + g, t] = value
-                    if again:
-                        vals[h * 2 + g, t + TABLES] = value
+        lax.fori_loop(0, NZC // 2, widen, 0)
+
+        def place_three(b, carry):
+            for r in range(3):
+                t = b * 3 + r
+                for h in range(2):
+                    at = place_s[t * 2 + h, 0]
+                    vals[h, t] = unit[at] * sc[q * 64 + at]
             return carry
 
-        lax.fori_loop(0, SHIFTS, functools.partial(place, again=True), 0)
-        lax.fori_loop(SHIFTS, TABLES, functools.partial(place, again=False), 0)
-
-        def shift(d, carry):
+        lax.fori_loop(0, TABLES // 3, place_three, 0)
+        for h in range(2):
+            vals[h, TABLES : TABLES + SHIFTS + 1] = vals[h, 0 : SHIFTS + 1]
+
+        def shift(e, carry):
+            d = e * 2
             for b in range(0, TABLES, 9):
-                total = acc[d, b : b + 9]
-                for k in range(4):
-                    total = total + vals[k, b : b + 9] * vals[k, pl.ds(d + 1 + b, 9)]
-                acc[d, b : b + 9] = total
+                one = acc[d, b : b + 9]
+                two = acc[d + 1, b : b + 9]
+                for h in range(2):
+                    left = vals[h, b : b + 9]
+                    right = vals[h, pl.ds(d + 1 + b, 10)]
+                    one = one + left * right[0:9]
+                    two = two + left * right[1:10]
+                acc[d, b : b + 9] = one
+                acc[d + 1, b : b + 9] = two
             return carry
 
-        lax.fori_loop(0, SHIFTS, shift, 0)
+        lax.fori_loop(0, (SHIFTS + 1) // 2, shift, 0)
 
     def layer(inputs, weight, bias):
         product = jnp.dot(inputs, weight[...], preferred_element_type=F32)
@@ -253,9 +289,9 @@
         hidden = layer(hidden, w2v, b2v)
         hidden = layer(hidden, w3v, b3v)
         hidden = layer(hidden, w4v, b4v)
-        last = jnp.broadcast_to(wout_ref[...].astype(F32), (8, 256)).astype(BF16)
+        last = jnp.broadcast_to(woutv[...].astype(F32).reshape(1, 256), (8, 256)).astype(BF16)
         final = lax.dot_general(last, hidden, (((1,), (1,)), ((), ())), preferred_element_type=F32)
-        lg[px, q] = final + bout_ref[0]
+        lg[px, q] = final
         for peer in x_peers:
             pltpu.make_async_remote_copy(
                 src_ref=lg.at[px, q],
@@ -283,17 +319,17 @@
         def _():
             spread_scales()
 
-        @pl.when(i >= LAG)
-        def _():
-            gram(i - LAG)
-
-        @pl.when((i >= LAG) & ((i - LAG) % NG == NG - 1))
-        def _():
-            finish((i - LAG) // NG)
+        @pl.when((i >= LAG) & ((i - LAG) % SPLIT == 0))
+        def _():
+            gram((i - LAG) // SPLIT)
+
+        @pl.when((i >= LAG) & ((i - LAG) % (NG * SPLIT) == (NG - 1) * SPLIT))
+        def _():
+            finish((i - LAG) // (NG * SPLIT))
 
         return carry
 
-    lax.fori_loop(0, CHUNKS + LAG, step, 0)
+    lax.fori_loop(0, CHUNKS + LAG - SPLIT + 1, step, 0)
 
     def sent(ch, carry):
         three = y_recv.at[ch, pl.ds(0, 3)]
@@ -315,40 +351,35 @@
 
 
 def per_device(codes, scales, shard_slot, w1, b1, w2, b2, w3, b3, w4, b4, wout, bout):
-    flat = shard_slot.reshape(-1)
-    spot = jnp.arange(flat.shape[0], dtype=jnp.int32)
-    half = flat.shape[0] // 2
-    merged_spot = spot % half
-    row, j = merged_spot // 2, merged_spot % 2
-    merged_spot = (row % NZC) * 4 + (row // NZC) * 2 + j
-    matches = flat[None, :] == jnp.arange(2 * TABLES, dtype=jnp.int32)[:, None]
-    place = jnp.sum(jnp.where(matches, merged_spot[None, :], 0), axis=1).astype(jnp.int32)
-
     codes = codes.reshape(2, 8, 8, NY * NZC, NQ, 128).transpose(0, 1, 3, 4, 2, 5)
     scales = scales.reshape(2, NY * NZC, NQ, 128).transpose(1, 2, 0, 3).reshape(NY * NZC, 8, 128)
 
     any_spec = pl.BlockSpec(memory_space=pl.ANY)
-    smem = pl.BlockSpec(memory_space=pltpu.SMEM)
     vmem = pl.BlockSpec(memory_space=pltpu.VMEM)
     dma = pltpu.SemaphoreType.DMA
-    return pl.pallas_call(
+    logits = pl.pallas_call(
         kernel,
         out_shape=jax.ShapeDtypeStruct((NX, NQ * 128), F32),
-        in_specs=[smem, smem, smem] + [any_spec] * 10 + [vmem],
+        in_specs=[any_spec] * 12,
         out_specs=vmem,
         scratch_shapes=[
-            pltpu.VMEM((CHUNKS, NY, 2, 2, NZC, 8, 128), BF16),
-            pltpu.VMEM((CHUNKS, NZC, 2, 2, 2, 8, 128), BF16),
-            pltpu.VMEM((CHUNKS, NZC, 2, 2, 2, 8, 128), BF16),
+            pltpu.VMEM((2, NY * NZC), jnp.int32),
+            pltpu.SMEM((2, NY * NZC), jnp.int32),
+            pltpu.VMEM((56, 128), jnp.int32),
+            pltpu.SMEM((56, 128), jnp.int32),
+            pltpu.VMEM(wout.shape, BF16),
+            pltpu.VMEM((CHUNKS, NY, J, NZC, 8, 128), BF16),
+            pltpu.VMEM((CHUNKS, NZC, 2, J, 8, 128), BF16),
+            pltpu.VMEM((CHUNKS, NZC, 2, J, 8, 128), BF16),
             pltpu.VMEM((NY * NZC, 8, 128), F32),
             pltpu.VMEM((NY * 8, 16, 128), BF16),
             pltpu.VMEM((NY, 8, 16, 128), BF16),
             pltpu.VMEM((8, 2, 16, 128), BF16),
             pltpu.VMEM((NZC, 16, 128), BF16),
             pltpu.VMEM((NQ * 64, 8, 128), F32),
-            pltpu.VMEM((64, 2, 8, 128), F32),
-            pltpu.VMEM((4, TABLES + SHIFTS, 8, 128), F32),
-            pltpu.VMEM((SHIFTS, TABLES, 8, 128), F32),
+            pltpu.VMEM((64, 8, 128), F32),
+            pltpu.VMEM((2, TABLES + SHIFTS + 1, 8, 128), F32),
+            pltpu.VMEM((SHIFTS + 1, TABLES, 8, 128), F32),
             pltpu.VMEM((SHIFTS * 32, 128), F32),
             pltpu.VMEM((NX, NQ, 8, 128), F32),
             pltpu.VMEM(w1.shape, BF16),
@@ -369,12 +400,14 @@
             dma((NQ,)),
             dma((NQ,)),
             dma,
-            dma((8,)),
+            dma((2,)),
+            dma((9,)),
         ],
         compiler_params=pltpu.CompilerParams(
             collective_id=0, has_side_effects=True, vmem_limit_bytes=56 * 1024 * 1024
         ),
-    )(flat, place, bout, codes, scales, w1, b1[None], w2, b2[None], w3, b3[None], w4, b4[None], wout[None])
+    )(shard_slot.T, codes, scales, w1, b1[None], w2, b2[None], w3, b3[None], w4, b4[None], wout)
+    return logits + bout
 
 
 def solution(mesh):

time: 125 us -> 119 us (0.952)
  local copies, waits for them, and re-layouts: 3.42 us -> 0 us
  Pallas kernels: 120 us -> 117 us
    pallas_call x1, Pallas kernels: 120 us -> 117 us  [per_device(): pl.pallas_call(kernel, out_shape=jax.ShapeDtypeStruct((NX, NQ * 128), F32...]
    unnamed x4 -> x0, local copies, waits for them, and re-layouts: 2.07 us -> none
    add x1, other arithmetic: 0.02 us -> 1.3 us  [per_device(): return logits + bout]
where the time goes in v2:
time: 119 us
  Pallas kernels  117 us (98%)
  other arithmetic  1.3 us (1%)
    pallas_call x1, Pallas kernels, per_device(): pl.pallas_call(kernel, out_shape=jax.ShapeDtypeStruct((NX, NQ * 128), F32...  117 us

profile of v2, /device:TPU:1, one launch (start us, length us, event | category | flops | bytes accessed | tf_op | source)
XLA Modules:
  0.0 118.6 jit_solution(5409070519111801739)
XLA Ops:
  0.7 116.7 %shard_map.127 = f32[4,512]{1,0:T(4,128)} custom-call(s32[2,64]{1,0:T(2,128)} %bitcast.20, bf16[2,8,64,4,8,128]{5,4,3,2,1,0:T(8,128)(2,1)} %bitcast.15, f32[64,8,128]{2,1,0:T(8,128)} %bitcast.16, bf16[351,1024]{1,0:T(8,128)(2,1)} %w1.1, f32[1,1024]{1,0:T(1,128)} %bitcast.17, bf16[1024,1024]{1,0:T(8,128)(2,1)} %w2.1, f32[1,1024]{1,0:T(1,128)} %bitcast.18, ...), custom_call_target="tpu_custom_call" | custom-call | tf_op jit(solution)/shard_map/pallas_call | solution.py:360
  117.3 1.3 %broadcast_add_fusion = f32[4,512]{1,0:T(4,128)} fusion(f32[4,512]{1,0:T(4,128)} %shard_map.127, f32[]{:T(128)} %bitcast.14), kind=kLoop, calls=%fused_computation | loop fusion | flops 2048 | bytes 16388 | tf_op jit(solution)/shard_map/add | solution.py:410

commit v3 on v2

v3 whole, which is shorter than its diff:
```python
import functools

import jax
import jax.numpy as jnp
from jax import lax
from jax.experimental import pallas as pl
from jax.experimental.pallas import tpu as pltpu
from jax.sharding import PartitionSpec as P

MESH = pl.DeviceIdType.MESH
F32 = jnp.float32
BF16 = jnp.bfloat16

TABLES = 27
SHIFTS = TABLES // 2
PAIRS = TABLES * SHIFTS
NY, NZC, NX = 4, 16, 4
NQ, NG = 4, 8
GROUPS = NQ * NG
CHUNKS = GROUPS - 1
AHEAD = 6
LAG = 3
Z_ORDER = (4, 3, 5, 2, 6, 1, 7)


def kernel(
    slots,
    codes,
    scales,
    w1,
    b1,
    w2,
    b2,
    w3,
    b3,
    w4,
    b4,
    wout,
    out_ref,
    slot_v,
    slot_s,
    place_v,
    place_s,
    woutv,
    y_recv,
    merged,
    z_recv,
    early,
    late,
    sc_in,
    rows,
    unit,
    vals,
    acc,
    xt,
    lg,
    w1v,
    w1p,
    b1v,
    w2v,
    b2v,
    w3v,
    b3v,
    w4v,
    b4v,
    y_ssem,
    y_rsem,
    z_ssem,
    z_rsem,
    row_sem,
    lg_ssem,
    lg_rsem,
    own_sem,
    side_sem,
    in_sem,
    slot_sem,
    w_sem,
):
    me = lax.axis_index("tbl")
    px = lax.axis_index("pair")
    y = me // NZC
    zc = me % NZC
    z = zc // 2
    core = zc % 2

    y_peers = [((y + k) % NY) for k in (1, 3, 2)]
    z_peers = [((z + dz) % 8) * 2 + c for dz in Z_ORDER for c in range(2)] + [z * 2 + (1 - core)]
    x_peers = [((px + k) % NX) for k in (1, 3, 2)]

    barrier = pltpu.get_barrier_semaphore()
    for peer in y_peers:
        pl.semaphore_signal(barrier, inc=1, device_id={"tbl": peer * NZC + zc}, device_id_type=MESH)
    for peer in z_peers:
        pl.semaphore_signal(barrier, inc=1, device_id={"tbl": y * NZC + peer}, device_id_type=MESH)
    for peer in x_peers:
        pl.semaphore_signal(barrier, inc=1, device_id={"pair": peer}, device_id_type=MESH)

    sc_load = pltpu.make_async_copy(scales, sc_in, in_sem)
    sc_load.start()

    def load_rows(n):
        return pltpu.make_async_copy(codes.at[:, n % NG, :, :, n // NG], rows.at[n], row_sem.at[n])

    load_rows(0).start()
    load_rows(CHUNKS).start()
    slot_loads = [
        pltpu.make_async_copy(slots, slot_v, slot_sem.at[0]),
        pltpu.make_async_copy(slots, slot_s, slot_sem.at[1]),
    ]
    for load in slot_loads:
        load.start()
    weights = ((w1, w1v), (b1, b1v), (w2, w2v), (b2, b2v), (w3, w3v), (b3, b3v), (w4, w4v), (b4, b4v), (wout, woutv))
    loads = [pltpu.make_async_copy(src, dst, w_sem.at[i]) for i, (src, dst) in enumerate(weights)]
    lax.fori_loop(1, AHEAD + 2, lambda n, carry: (load_rows(n).start(), carry)[1], 0)
    for load in loads:
        load.start()


    def dequantize(n):
        load_rows(n).wait()
        q = n // NG

        def body(k, carry):
            for j in range(2):
                factor = sc_in[pl.ds(k * NZC, NZC), pl.ds(q * 2 + j, 1)]
                rows[n, j, k] = (rows[n, j, k].astype(F32) * factor).astype(BF16)
            return carry

        lax.fori_loop(0, NY, body, 0)

        @pl.when(n < CHUNKS)
        def _():
            y_recv[n, y] = rows[n, :, y]

    sc_load.wait()
    dequantize(0)
    pl.semaphore_wait(barrier, len(y_peers) + len(z_peers) + len(x_peers))

    def send_y(ch):
        for peer in y_peers:
            pltpu.make_async_remote_copy(
                src_ref=rows.at[ch, :, peer],
                dst_ref=y_recv.at[ch, y],
                send_sem=y_ssem.at[ch],
                recv_sem=y_rsem.at[ch],
                device_id={"tbl": peer * NZC + zc},
                device_id_type=MESH,
            ).start()

    send_y(0)
    dequantize(CHUNKS)

    for peer in z_peers:
        pltpu.make_async_remote_copy(
            src_ref=rows.at[CHUNKS, :, :, peer],
            dst_ref=early.at[zc],
            send_sem=side_sem.at[0],
            recv_sem=side_sem.at[1],
            device_id={"tbl": y * NZC + peer},
            device_id_type=MESH,
        ).start()
    early[zc] = rows[CHUNKS, :, :, zc]

    def send_late():
        pltpu.make_async_copy(early.at[pl.ds(0, NZC - 1)], early.at[pl.ds(0, NZC - 1)], side_sem.at[1]).wait()
        for peer in y_peers:
            pltpu.make_async_remote_copy(
                src_ref=early.at[:, :, peer],
                dst_ref=late.at[y],
                send_sem=side_sem.at[2],
                recv_sem=side_sem.at[3],
                device_id={"tbl": peer * NZC + zc},
                device_id_type=MESH,
            ).start()
        late[y] = early[:, :, y]


    for ch in range(1, AHEAD):
        dequantize(ch)
        send_y(ch)
    lax.fori_loop(AHEAD + 2, CHUNKS, lambda n, carry: (load_rows(n).start(), carry)[1], 0)
    dequantize(AHEAD)

    for load in loads:
        load.wait()
    row = lax.broadcasted_iota(jnp.int32, (SHIFTS * 32, PAIRS), 0)
    col = lax.broadcasted_iota(jnp.int32, (SHIFTS * 32, PAIRS), 1)
    first = row % 32
    second = first + row // 32 + 1
    second = jnp.where(second >= TABLES, second - TABLES, second)
    low = jnp.minimum(first, second)
    high = jnp.maximum(first, second)
    rank = low * TABLES - (low * (low + 1)) // 2 + high - low - 1
    chosen = jnp.where((rank == col) & (first < TABLES), 1.0, 0.0).astype(BF16)
    w1p[...] = jnp.dot(chosen, w1v[...], preferred_element_type=F32).astype(BF16)
    xt[...] = jnp.zeros_like(xt)
    acc[...] = jnp.zeros_like(acc)

    for load in slot_loads:
        load.wait()
    shard = lax.broadcasted_iota(jnp.int32, (56, NY * NZC), 0)
    table_row = lax.broadcasted_iota(jnp.int32, (56, NY * NZC), 1) % (2 * NZC)
    spot = table_row % NZC * 4 + table_row // NZC * 2
    place = jnp.zeros((56, 1), jnp.int32)
    for j in range(2):
        here = jnp.broadcast_to(slot_v[j : j + 1], shard.shape) == shard
        found = jnp.max(jnp.where(here, spot + j, 0), axis=1, keepdims=True)
        place = jnp.maximum(place, found)
    place_v[...] = jnp.broadcast_to(place, (56, 128))
    place_copy = pltpu.make_async_copy(place_v, place_s, slot_sem.at[0])
    place_copy.start()
    place_copy.wait()
    flags = [[slot_s[j, p * NZC + zc] for j in range(2)] for p in range(2)]

    def merge(ch):
        three = y_recv.at[ch, pl.ds(0, 3)]
        pltpu.make_async_copy(three, three, y_rsem.at[ch]).wait()
        for p in range(2):
            for j in range(2):
                merged[ch, :, p, j] = jnp.where(flags[p][j] >= 0, y_recv[ch, p, j], y_recv[ch, p + 2, j])
        for peer in z_peers:
            pltpu.make_async_remote_copy(
                src_ref=merged.at[ch, peer],
                dst_ref=z_recv.at[ch, zc],
                send_sem=z_ssem.at[ch],
                recv_sem=z_rsem.at[ch],
                device_id={"tbl": y * NZC + peer},
                device_id_type=MESH,
            ).start()
        z_recv[ch, zc] = merged[ch, zc]

    def gram(n):
        @pl.when(n != CHUNKS - 1)
        def _():
            ch = jnp.minimum(n, CHUNKS - 1)
            most = z_recv.at[ch, pl.ds(0, NZC - 1)]
            pltpu.make_async_copy(most, most, z_rsem.at[ch]).wait()

            def widen(s, carry):
                for half in range(2):
                    for p in range(2):
                        for j in range(2):
                            unit[s * 8 + half * 4 + p * 2 + j] = z_recv[ch, s * 2 + half, p, j].astype(F32)
                return carry

            lax.fori_loop(0, NZC // 2, widen, 0)

        @pl.when(n == CHUNKS - 1)
        def _():
            pltpu.make_async_copy(late.at[pl.ds(0, 3)], late.at[pl.ds(0, 3)], side_sem.at[3]).wait()

            def pick(s, carry):
                for p in range(2):
                    for j in range(2):
                        take_low = slot_s[j, p * NZC + s] >= 0
                        unit[s * 4 + p * 2 + j] = jnp.where(take_low, late[p, s, j], late[p + 2, s, j]).astype(F32)
                return carry

            lax.fori_loop(0, NZC, pick, 0)

        def place_three(b, carry):
            for r in range(3):
                t = b * 3 + r
                for h in range(2):
                    at = place_s[t * 2 + h, 0]
                    vals[h, t] = unit[at]
            return carry

        lax.fori_loop(0, TABLES // 3, place_three, 0)
        for h in range(2):
            vals[h, TABLES : TABLES + SHIFTS + 1] = vals[h, 0 : SHIFTS + 1]

        def shift(e, carry):
            d = e * 2
            for b in range(0, TABLES, 9):
                one = acc[d, b : b + 9]
                two = acc[d + 1, b : b + 9]
                for h in range(2):
                    left = vals[h, b : b + 9]
                    right = vals[h, pl.ds(d + 1 + b, 10)]
                    one = one + left * right[0:9]
                    two = two + left * right[1:10]
                acc[d, b : b + 9] = one
                acc[d + 1, b : b + 9] = two
            return carry

        lax.fori_loop(0, (SHIFTS + 1) // 2, shift, 0)

    def layer(inputs, weight, bias):
        product = jnp.dot(inputs, weight[...], preferred_element_type=F32)
        return jnp.maximum(product + bias[...], 0.0).astype(BF16)

    sub = lax.broadcasted_iota(jnp.int32, (8, 128), 0)

    def fold_rows(rows):
        for dist in (4, 2, 1):
            low = (sub & dist) == 0
            merged_rows = []
            for a in range(dist):
                one, two = rows[a], rows[a + dist]
                if one is None:
                    merged_rows.append(None)
                    continue
                two = jnp.zeros_like(one) if two is None else two
                other = jnp.where(low, two, one)
                if dist == 4:
                    moved = pltpu.roll(other, 4, 0)
                else:
                    moved = jnp.where(low, pltpu.roll(other, 8 - dist, 0), pltpu.roll(other, dist, 0))
                merged_rows.append(jnp.where(low, one, two) + moved)
            rows = merged_rows
        return rows[0]

    def finish(q):
        def fold(d, carry):
            for b in range(0, 32, 8):
                rows = [acc[d, b + r] if b + r < TABLES else None for r in range(8)]
                xt[pl.ds(pl.multiple_of(d * 32 + b, 8), 8)] = fold_rows(rows)
            acc[d] = jnp.zeros((TABLES, 8, 128), F32)
            return carry

        lax.fori_loop(0, SHIFTS, fold, 0)
        hidden = xt[...].T.astype(BF16)
        hidden = layer(hidden, w1p, b1v)
        hidden = layer(hidden, w2v, b2v)
        hidden = layer(hidden, w3v, b3v)
        hidden = layer(hidden, w4v, b4v)
        last = jnp.broadcast_to(woutv[...].astype(F32).reshape(1, 256), (8, 256)).astype(BF16)
        final = lax.dot_general(last, hidden, (((1,), (1,)), ((), ())), preferred_element_type=F32)
        lg[q] = final[0:1]
        pltpu.make_async_copy(lg.at[q], out_ref.at[q, px], own_sem.at[q]).start()
        for peer in x_peers:
            pltpu.make_async_remote_copy(
                src_ref=lg.at[q],
                dst_ref=out_ref.at[q, px],
                send_sem=lg_ssem.at[q],
                recv_sem=lg_rsem.at[q],
                device_id={"pair": peer},
                device_id_type=MESH,
            ).start()

    def step(i, carry):
        @pl.when(i < CHUNKS)
        def _():
            merge(i)

        @pl.when(i + AHEAD < CHUNKS)
        def _():
            send_y(i + AHEAD)

        @pl.when(i + AHEAD + 1 < CHUNKS)
        def _():
            dequantize(i + AHEAD + 1)

        @pl.when(i + AHEAD == CHUNKS)
        def _():
            send_late()

        @pl.when(i >= LAG)
        def _():
            gram(i - LAG)

        @pl.when((i >= LAG) & ((i - LAG) % NG == NG - 1))
        def _():
            finish((i - LAG) // NG)

        return carry

    lax.fori_loop(0, GROUPS + LAG, step, 0)

    def sent(ch, carry):
        three = y_recv.at[ch, pl.ds(0, 3)]
        pltpu.make_async_copy(three, three, y_ssem.at[ch]).wait()
        most = z_recv.at[ch, pl.ds(0, NZC - 1)]
        pltpu.make_async_copy(most, most, z_ssem.at[ch]).wait()
        return carry

    lax.fori_loop(0, CHUNKS, sent, 0)
    pltpu.make_async_copy(early.at[pl.ds(0, NZC - 1)], early.at[pl.ds(0, NZC - 1)], side_sem.at[0]).wait()
    pltpu.make_async_copy(late.at[pl.ds(0, 3)], late.at[pl.ds(0, 3)], side_sem.at[2]).wait()
    for q in range(NQ):
        three = out_ref.at[q, pl.ds(0, 3)]
        pltpu.make_async_copy(three, three, lg_ssem.at[q]).wait()
        pltpu.make_async_copy(lg.at[q], out_ref.at[q, px], own_sem.at[q]).wait()
        pltpu.make_async_copy(three, three, lg_rsem.at[q]).wait()


def per_device(codes, scales, shard_slot, w1, b1, w2, b2, w3, b3, w4, b4, wout, bout):
    codes = codes.reshape(2, NG, 8, NY, NZC, NQ, 128).transpose(0, 1, 3, 4, 5, 2, 6)
    scales = scales.reshape(2, NY * NZC, NQ, 128).transpose(1, 2, 0, 3).reshape(NY * NZC, 8, 128)

    any_spec = pl.BlockSpec(memory_space=pl.ANY)
    dma = pltpu.SemaphoreType.DMA
    logits = pl.pallas_call(
        kernel,
        out_shape=jax.ShapeDtypeStruct((NQ, NX, 1, 128), F32),
        in_specs=[any_spec] * 12,
        out_specs=any_spec,
        scratch_shapes=[
            pltpu.VMEM((2, NY * NZC), jnp.int32),
            pltpu.SMEM((2, NY * NZC), jnp.int32),
            pltpu.VMEM((56, 128), jnp.int32),
            pltpu.SMEM((56, 128), jnp.int32),
            pltpu.VMEM(wout.shape, BF16),
            pltpu.VMEM((CHUNKS, NY, 2, NZC, 8, 128), BF16),
            pltpu.VMEM((CHUNKS, NZC, 2, 2, 8, 128), BF16),
            pltpu.VMEM((CHUNKS, NZC, 2, 2, 8, 128), BF16),
            pltpu.VMEM((NZC, 2, NY, 8, 128), BF16),
            pltpu.VMEM((NY, NZC, 2, 8, 128), BF16),
            pltpu.VMEM((NY * NZC, 8, 128), F32),
            pltpu.VMEM((GROUPS, 2, NY, NZC, 8, 128), BF16),
            pltpu.VMEM((64, 8, 128), F32),
            pltpu.VMEM((2, TABLES + SHIFTS + 1, 8, 128), F32),
            pltpu.VMEM((SHIFTS + 1, TABLES, 8, 128), F32),
            pltpu.VMEM((SHIFTS * 32, 128), F32),
            pltpu.VMEM((NQ, 1, 128), F32),
            pltpu.VMEM(w1.shape, BF16),
            pltpu.VMEM((SHIFTS * 32, w1.shape[1]), BF16),
            pltpu.VMEM((1, b1.shape[0]), F32),
            pltpu.VMEM(w2.shape, BF16),
            pltpu.VMEM((1, b2.shape[0]), F32),
            pltpu.VMEM(w3.shape, BF16),
            pltpu.VMEM((1, b3.shape[0]), F32),
            pltpu.VMEM(w4.shape, BF16),
            pltpu.VMEM((1, b4.shape[0]), F32),
            dma((CHUNKS,)),
            dma((CHUNKS,)),
            dma((CHUNKS,)),
            dma((CHUNKS,)),
            dma((GROUPS,)),
            dma((NQ,)),
            dma((NQ,)),
            dma((NQ,)),
            dma((4,)),
            dma,
            dma((2,)),
            dma((9,)),
        ],
        compiler_params=pltpu.CompilerParams(
            collective_id=0, has_side_effects=True, vmem_limit_bytes=56 * 1024 * 1024
        ),
    )(shard_slot.T, codes, scales, w1, b1[None], w2, b2[None], w3, b3[None], w4, b4[None], wout)
    return logits.transpose(1, 2, 0, 3).reshape(NX, NQ * 128) + bout


def solution(mesh):
    return jax.shard_map(
        per_device,
        mesh=mesh,
        in_specs=(P("tbl", None, "pair"), P("tbl", "pair")) + (P(),) * 11,
        out_specs=P(None, "tbl"),
        check_vma=False,
    )
```

time: 119 us -> 114 us (0.958)
  Pallas kernels: 117 us -> 112 us
    pallas_call x1, Pallas kernels: 117 us -> 112 us  [per_device(): pl.pallas_call(kernel, out_shape=jax.ShapeDtypeStruct((NQ, NX, 1, 128), F...]
where the time goes in v3:
time: 114 us
  Pallas kernels  112 us (98%)
  other arithmetic  1.3 us (1%)
    pallas_call x1, Pallas kernels, per_device(): pl.pallas_call(kernel, out_shape=jax.ShapeDtypeStruct((NQ, NX, 1, 128), F...  112 us

profile of v3, /device:TPU:1, one launch (start us, length us, event | category | flops | bytes accessed | tf_op | source)
XLA Modules:
  0.0 113.8 jit_solution(8929734408569886338)
XLA Ops:
  0.7 111.9 %shard_map.127 = f32[4,4,1,128]{3,2,1,0:T(1,128)} custom-call(s32[2,64]{1,0:T(2,128)} %bitcast.23, bf16[2,8,4,16,4,8,128]{6,5,4,3,2,1,0:T(8,128)(2,1)} %bitcast.18, f32[64,8,128]{2,1,0:T(8,128)} %bitcast.19, bf16[351,1024]{1,0:T(8,128)(2,1)} %w1.1, f32[1,1024]{1,0:T(1,128)} %bitcast.20, bf16[1024,1024]{1,0:T(8,128)(2,1)} %w2.1, f32[1,1024]{1,0:T(1,128)} %bitcast.21, ...), custom_call_target="tpu_custom_call" | custom-call | tf_op jit(solution)/shard_map/pallas_call | solution.py:394
  112.5 1.3 %broadcast_add_fusion = f32[4,4,1,128]{3,2,1,0:T(1,128)} fusion(f32[4,4,1,128]{3,2,1,0:T(1,128)} %shard_map.127, f32[]{:T(128)} %bitcast.17), kind=kLoop, calls=%fused_computation | loop fusion | flops 2048 | bytes 16388 | tf_op jit(solution)/shard_map/add | solution.py:443

commit v4 on v3

--- a/solution.py
+++ b/solution.py
@@ -70,7 +70,6 @@
     row_sem,
     lg_ssem,
     lg_rsem,
-    own_sem,
     side_sem,
     in_sem,
     slot_sem,
@@ -134,6 +133,7 @@
 
     sc_load.wait()
     dequantize(0)
+    dequantize(CHUNKS)
     pl.semaphore_wait(barrier, len(y_peers) + len(z_peers) + len(x_peers))
 
     def send_y(ch):
@@ -148,7 +148,6 @@
             ).start()
 
     send_y(0)
-    dequantize(CHUNKS)
 
     for peer in z_peers:
         pltpu.make_async_remote_copy(
@@ -328,7 +327,7 @@
         last = jnp.broadcast_to(woutv[...].astype(F32).reshape(1, 256), (8, 256)).astype(BF16)
         final = lax.dot_general(last, hidden, (((1,), (1,)), ((), ())), preferred_element_type=F32)
         lg[q] = final[0:1]
-        pltpu.make_async_copy(lg.at[q], out_ref.at[q, px], own_sem.at[q]).start()
+        out_ref[q, px] = final[0:1]
         for peer in x_peers:
             pltpu.make_async_remote_copy(
                 src_ref=lg.at[q],
@@ -381,7 +380,6 @@
     for q in range(NQ):
         three = out_ref.at[q, pl.ds(0, 3)]
         pltpu.make_async_copy(three, three, lg_ssem.at[q]).wait()
-        pltpu.make_async_copy(lg.at[q], out_ref.at[q, px], own_sem.at[q]).wait()
         pltpu.make_async_copy(three, three, lg_rsem.at[q]).wait()
 
 
@@ -393,9 +391,9 @@
     dma = pltpu.SemaphoreType.DMA
     logits = pl.pallas_call(
         kernel,
-        out_shape=jax.ShapeDtypeStruct((NQ, NX, 1, 128), F32),
+        out_shape=pltpu.VMEM((NQ, NX, 1, 128), F32),
         in_specs=[any_spec] * 12,
-        out_specs=any_spec,
+        out_specs=pl.BlockSpec(memory_space=pltpu.VMEM),
         scratch_shapes=[
             pltpu.VMEM((2, NY * NZC), jnp.int32),
             pltpu.SMEM((2, NY * NZC), jnp.int32),
@@ -430,7 +428,6 @@
             dma((GROUPS,)),
             dma((NQ,)),
             dma((NQ,)),
-            dma((NQ,)),
             dma((4,)),
             dma,
             dma((2,)),

time: 114 us -> 113 us (level)
  no operation moved by 1% of the time
where the time goes in v4:
time: 113 us
  Pallas kernels  112 us (99%)
    pallas_call x1, Pallas kernels, per_device(): pl.pallas_call(kernel, out_shape=pltpu.VMEM((NQ, NX, 1, 128), F32), in_sp...  112 us

profile of v4, /device:TPU:1, one launch (start us, length us, event | category | flops | bytes accessed | tf_op | source)
XLA Modules:
  0.0 113.1 jit_solution(4378580685700197521)
XLA Ops:
  0.7 111.9 %shard_map.127 = f32[4,4,1,128]{3,2,1,0:T(1,128)S(1)} custom-call(s32[2,64]{1,0:T(2,128)} %bitcast.23, bf16[2,8,4,16,4,8,128]{6,5,4,3,2,1,0:T(8,128)(2,1)} %bitcast.18, f32[64,8,128]{2,1,0:T(8,128)} %bitcast.19, bf16[351,1024]{1,0:T(8,128)(2,1)} %w1.1, f32[1,1024]{1,0:T(1,128)} %bitcast.20, bf16[1024,1024]{1,0:T(8,128)(2,1)} %w2.1, f32[1,1024]{1,0:T(1,128)} %bitcast.21, ...), custom_call_target="tpu_custom_call" | custom-call | tf_op jit(solution)/shard_map/pallas_call | solution.py:392
  112.5 0.6 broadcast_add_fusion
